TPU v7x, 32 devices: a 4x4x1 block of a 4x4x8 slice. The times are simulated.
32 devices in a mesh: dp: 1 (over z), vp: 32 (over y, x, core).
Axes of the slice: x: 4, y: 4, z: 1, core: 2. Of those that a mesh axis runs over, the one named last changes fastest.
The devices are a block of a 4x4x8 slice.
Arguments:
- hidden: bfloat16 [384, 5120], P('dp')
- w_head: bfloat16 [5120, 131072], P(None, 'vp')
- inv_temp: float32 [384], P('dp')
- target_ids: int32 [384], P('dp')
Outputs:
- output 1: float32 [384, 131072], P(('dp', 'vp'))
- output 2: float32 [384], P('dp')
All inputs are finite; a program needn't handle non-finite values.
Results may differ from a plain program's by a relative error of at most 0.001.
Values are sent between devices in bfloat16 or wider.
A program may use at most 768 MiB of HBM per device.

v0:
```python
import jax
import jax.numpy as jnp
from jax import lax
from jax.sharding import PartitionSpec as P, NamedSharding


def solution(mesh):
    group_size = mesh.shape["vp"]

    def local_step(hidden, w_local, inv_temp, target_ids):
        group_index = lax.axis_index("vp")
        local_vocab = w_local.shape[1]
        logits = jnp.dot(hidden, w_local, preferred_element_type=jnp.float32)
        scaled = logits * inv_temp[:, None]
        local_max = jnp.max(scaled, axis=1)
        exp_vals = jnp.exp(scaled - local_max[:, None])
        local_sum = jnp.sum(exp_vals, axis=1)
        shard_stats = lax.all_gather(jnp.stack([local_max, local_sum]), "vp")
        global_max = jnp.max(shard_stats[:, 0], axis=0)
        global_sum = jnp.sum(shard_stats[:, 1] * jnp.exp(shard_stats[:, 0] - global_max[None, :]), axis=0)
        row_scale = jnp.exp(local_max - global_max) / global_sum
        local_cdf = jnp.cumsum(exp_vals * row_scale[:, None], axis=1)
        totals = lax.all_gather(local_cdf[:, -1], "vp")
        earlier = (jnp.arange(group_size) < group_index)[:, None]
        offset = jnp.sum(jnp.where(earlier, totals, 0.0), axis=0)
        cdf_cols = local_cdf + offset[:, None]
        local_ids = target_ids - group_index * local_vocab
        in_shard = (local_ids >= 0) & (local_ids < local_vocab)
        picked = jnp.take_along_axis(cdf_cols, jnp.clip(local_ids, 0, local_vocab - 1)[:, None], axis=1)[:, 0]
        cdf_at_target = lax.psum(jnp.where(in_shard, picked, 0.0), "vp")
        cdf_rows = lax.all_to_all(cdf_cols, "vp", 0, 1, tiled=True)
        return cdf_rows, cdf_at_target

    return jax.shard_map(
        local_step,
        mesh=mesh,
        in_specs=(P("dp", None), P(None, "vp"), P("dp"), P("dp")),
        out_specs=(P(("dp", "vp"), None), P("dp")),
        check_vma=False,
    )
```

profile of v0, /device:TPU:97, one launch (start us, length us, event | category | flops | bytes accessed | tf_op | source)
XLA Modules:
  0.0 326.1 jit_solution(12810387648220846816)
XLA Ops:
  0.6 26.5 %fusion.8 = (f32[384]{0:T(512)S(1)}, f32[384,4096]{1,0:T(8,128)}) fusion(f32[384]{0:T(512)} %param.6, bf16[384,5120]{1,0:T(8,128)(2,1)} %param.4, bf16[5120,4096]{1,0:T(8,128)(2,1)} %param.5), kind=kOutput, calls=%fused_computation.28 | convolution fusion | flops 16109273088 | bytes 52169728 | tf_op jit(solution)/shard_map/dot_general | solution.py:13
  27.2 0.0 copy-start.2
  27.2 3.9 %fusion = f32[384]{0:T(512)S(1)} fusion(f32[384,4096]{1,0:T(8,128)} %get-tuple-element.6, f32[384]{0:T(512)S(1)} %get-tuple-element.5), kind=kLoop, calls=%fused_computation.4 | loop fusion | flops 3145344 | bytes 6294528 | tf_op jit(solution)/shard_map/reduce_sum | solution.py:17
  31.1 31.9 %all-gather.2 = f32[32,2,384]{2,1,0:T(2,128)S(1)} all-gather(f32[1,2,384]{2,1,0:T(2,128)S(1)} %maximum_bitcast_fusion), channel_id=2, replica_groups=mesh['dp'=1,'vp'=32] {'vp'}, dimensions={0}, use_global_device_ids=true | all-gather | bytes 101376 | tf_op jit(solution)/shard_map/all_gather | solution.py:18
  63.0 0.1 slice_reduce_fusion
  63.2 0.0 copy-done.2
  63.2 1.4 multiply_bitcast_fusion
  64.6 4.0 %copy.24 = f32[48,8,32,128]{3,2,1,0:T(8,128)} copy(f32[48,8,32,128]{3,1,2,0:T(8,128)S(1)} %multiply_bitcast_fusion) | data formatting | bytes 12582912
  68.6 6.7 %copy.18 = f32[384,32,128]{0,1,2:T(8,128)} copy(f32[384,32,128]{2,1,0:T(8,128)} %bitcast.33) | data formatting | bytes 12582912 | tf_op jit(solution)/shard_map/reshape.2
  75.3 3.2 fusion.9
  78.5 0.0 copy-start.1
  78.5 2.7 copy-done.1
  81.2 0.1 reduce-window.9
  81.3 3.5 %broadcast_add_fusion.2 = f32[384,32,128]{0,1,2:T(8,128)S(1)} fusion(f32[384,32,128]{0,1,2:T(8,128)} %copy-done.1, f32[384,32]{0,1:T(8,128)S(1)} %slice.26), kind=kLoop, calls=%fused_computation.7 | loop fusion | flops 1572864 | bytes 12632064 | tf_op jit(solution)/shard_map/reduce_window_sum
  84.8 0.0 copy-start
  84.8 2.7 copy-done
  87.5 6.4 %copy.20 = f32[384,32,128]{0,2,1:T(8,128)} copy(f32[384,32,128]{0,1,2:T(8,128)S(1)} %broadcast_add_fusion.2) | data formatting | bytes 12582912 | tf_op jit(solution)/shard_map/reduce_window_sum
  93.8 6.7 %copy.19 = f32[384,32,128]{2,1,0:T(8,128)} copy(f32[384,32,128]{0,1,2:T(8,128)} %copy-done) | data formatting | bytes 12582912 | tf_op jit(solution)/shard_map/reduce_window_sum
  100.6 0.7 slice.27
  101.3 32.3 %all-gather.1 = f32[12288,1]{0,1:T(1,128)S(1)} all-gather(f32[384,1]{0,1:T(1,128)S(1)} %slice.27), channel_id=3, replica_groups=mesh['dp'=1,'vp'=32] {'vp'}, dimensions={0}, use_global_device_ids=true | all-gather | bytes 50688 | tf_op jit(solution)/shard_map/all_gather | solution.py:23
  133.6 0.5 broadcast.51
  134.1 0.8 reduce.6
  134.9 7.9 %reduce_window_sum.20 = f32[32,12,4096]{2,1,0:T(8,128)} reshape(f32[384,32,128]{2,1,0:T(8,128)} %copy.19) | data formatting | bytes 12582912 | tf_op jit(solution)/shard_map/reduce_window_sum
  142.8 0.1 select_reduce_fusion
  142.9 0.1 add.24
  143.0 8.1 %broadcast_add_fusion = f32[32,12,4096]{2,1,0:T(8,128)} fusion(f32[32,12,4096]{2,1,0:T(8,128)} %reduce_window_sum.20, f32[32,12]{1,0:T(8,128)S(1)} %add.24), kind=kLoop, calls=%fused_computation.5 | loop fusion | flops 1572864 | bytes 12584448 | tf_op jit(solution)/shard_map/add | solution.py:26
  151.2 0.0 copy-start.3
  151.2 10.1 %all-to-all-start = ((f32[32,12,4096]{2,1,0:T(8,128)}), f32[32,12,4096]{2,1,0:T(8,128)}, u32[]{:S(2)}, u32[]{:S(2)}) async-start(f32[32,12,4096]{2,1,0:T(8,128)} %broadcast_add_fusion), calls=%async_computation | async-start | bytes 16777216 | tf_op jit(solution)/shard_map/all_to_all | solution.py:31
  161.3 0.0 copy-done.3
  161.4 5.8 %broadcast_add_fusion.1 = f32[384,4096]{0,1:T(8,128)} fusion(f32[384]{0:T(512)S(1)} %select_reduce_fusion, f32[384,32,128]{0,2,1:T(8,128)} %copy.20), kind=kLoop, calls=%fused_computation.6 | loop fusion | flops 1572864 | bytes 12584448 | tf_op jit(solution)/shard_map/add | solution.py:26
  167.2 14.5 %gather_fusion = f32[384]{0:T(512)S(1)} fusion(f32[384,4096]{0,1:T(8,128)} %broadcast_add_fusion.1, s32[384]{0:T(512)S(1)} %fusion.7), kind=kCustom, calls=%fused_computation | custom fusion | bytes 6144 | tf_op jit(solution)/shard_map/jit(take_along_axis)/gather | solution.py:29
  181.7 128.0 %psum.7 = f32[384]{0:T(512)} all-reduce(f32[384]{0:T(512)S(1)} %select_select_fusion), channel_id=1, replica_groups=mesh['dp'=1,'vp'=32] {'vp'}, use_global_device_ids=true, to_apply=%region_7.8 | all-reduce | flops 384 | bytes 3072 | tf_op jit(solution)/shard_map/psum | solution.py:30
  309.7 0.0 all-to-all-done
  309.7 7.0 %copy.21 = f32[12,32,4096]{2,1,0:T(8,128)S(1)} copy(f32[12,32,4096]{2,0,1:T(8,128)} %bitcast.4) | data formatting | bytes 12582912 | tf_op jit(solution)/shard_map/all_to_all | solution.py:31
  316.7 1.1 pad.4
  317.8 8.3 %copy.25 = f32[2,8,32,4096]{3,1,2,0:T(8,128)} copy(f32[2,8,32,4096]{3,2,1,0:T(8,128)S(1)} %bitcast.31) | data formatting | bytes 16777216
  (15 shorter events, 0.2 us)
Async XLA Ops:
  27.2 36.0 %copy-start.2 = (f32[384,4096]{1,0:T(8,128)S(1)}, f32[384,4096]{1,0:T(8,128)}, u32[]{:S(2)}) copy-start(f32[384,4096]{1,0:T(8,128)} %get-tuple-element.6) | copy-start | bytes 18874372
  78.5 2.7 copy-start.1
  84.8 2.7 copy-start
  151.2 10.1 %copy-start.3 = (s32[384]{0:T(512)S(1)}, s32[384]{0:T(512)}, u32[]{:S(2)}) copy-start(s32[384]{0:T(512)} %param.7) | copy-start | bytes 4612
  151.2 158.5 %all-to-all-start = ((f32[32,12,4096]{2,1,0:T(8,128)}), f32[32,12,4096]{2,1,0:T(8,128)}, u32[]{:S(2)}, u32[]{:S(2)}) async-start(f32[32,12,4096]{2,1,0:T(8,128)} %broadcast_add_fusion), calls=%async_computation | async-start | bytes 16777216 | tf_op jit(solution)/shard_map/all_to_all | solution.py:31
where the time goes:
time: 327 us; the launch traced here: 326 us
  blocking collectives  192 us (59%)
  local copies, waits for them, and re-layouts  69.3 us (21%)
  other arithmetic  27.1 us (8%)
  matrix products  26.5 us (8%)
  starting transfers between devices  10.1 us (3%)
    psum x1, blocking collectives, local_step(): cdf_at_target = lax.psum(jnp.where(in_shard, picked, 0.0), 'vp')  128 us
    all_gather x1, blocking collectives, local_step(): totals = lax.all_gather(local_cdf[:, -1], 'vp')  32.3 us
    all_gather x1, blocking collectives, local_step(): shard_stats = lax.all_gather(jnp.stack([local_max, local_sum]), 'vp')  31.9 us
    another operation x6, local copies, waits for them, and re-layouts  27.7 us
    dot_general x1, matrix products, local_step(): logits = jnp.dot(hidden, w_local, preferred_element_type=jnp.float32)  26.5 us
    unnamed x12, local copies, waits for them, and re-layouts  18.8 us
    gather x1, local copies, waits for them, and re-layouts, local_step(): jnp.take_along_axis(cdf_cols, jnp.clip(local_ids, 0, local_vocab - 1)[:,...  14.5 us
    add x2, other arithmetic, local_step(): cdf_cols = local_cdf + offset[:, None]  13.9 us
  transfers between devices with their start and end apart: 1, of which 0 were waited for; matrix products, arithmetic and copies ran while one was open for 6% of the time, Pallas kernels for 0%

commit v1 on v0

v1 whole, which is shorter than its diff:
```python
import functools
import math

import jax
import jax.numpy as jnp
from jax import lax
from jax.experimental import pallas as pl
from jax.experimental.pallas import tpu as pltpu
from jax.sharding import PartitionSpec as P

MESH = pl.DeviceIdType.MESH
SUB = 4
LANES = 128
TILE = 256
SLOTS = 4
LOW = -3.0e38


def torus_offsets(side):
    near = sorted(
        ((dy, dx) for dy in range(side) for dx in range(side)),
        key=lambda o: (min(o[0], side - o[0]) + min(o[1], side - o[1])),
    )
    return near[1:] + near[:1]


def kernel(n, hid_hbm, w_hbm, inv_ref, tgt_ref, out_ref, pick_ref, hid, wbuf, send, recv, invcol, tcol, tri, stat,
           stat_out, stat_in, scale, offset, tval, tall, hsem, wsem, ssem, rsem, stat_ss, stat_rs, t_ss, t_rs):
    me = lax.axis_index("vp")
    rows, depth = hid.shape
    local_vocab = w_hbm.shape[1]
    tiles = local_vocab // TILE
    own_groups = rows // n // SUB
    width = 2 * tiles + 8
    side = math.isqrt(n // 2)
    core, x, y = me % 2, (me // 2) % side, me // (2 * side)

    def w_copy(t):
        return pltpu.make_async_copy(w_hbm.at[:, pl.ds(pl.multiple_of(t * TILE, TILE), TILE)], wbuf.at[t % SLOTS], wsem.at[t % SLOTS])

    hid_copy = pltpu.make_async_copy(hid_hbm, hid, hsem)
    hid_copy.start()
    for t in range(SLOTS - 1):
        w_copy(t).start()

    barrier = pltpu.get_barrier_semaphore()

    def knock(d, c):
        pl.semaphore_signal(barrier, inc=1, device_id={"vp": lax.rem(me + d, n)}, device_id_type=MESH)
        return c

    lax.fori_loop(1, n, knock, 0)

    eye = lax.broadcasted_iota(jnp.int32, (LANES, LANES), 0) == lax.broadcasted_iota(jnp.int32, (LANES, LANES), 1)
    shard_start = (me * local_vocab).astype(jnp.float32)
    for q in range(rows // LANES):
        cut = slice(q * LANES, (q + 1) * LANES)
        for src, dst, base in ((inv_ref, invcol, 0.0), (tgt_ref, tcol, shard_start)):
            seg = jnp.broadcast_to(src[:, cut].astype(jnp.float32), (LANES, LANES))
            col = jnp.sum(jnp.where(eye, seg, 0.0), axis=1, keepdims=True) - base
            dst[cut, :] = jnp.broadcast_to(col, (LANES, LANES))
    tri[...] = (lax.broadcasted_iota(jnp.int32, (TILE, TILE), 0) <= lax.broadcasted_iota(jnp.int32, (TILE, TILE), 1)).astype(jnp.float32).astype(jnp.bfloat16)
    stat[...] = jnp.zeros_like(stat)

    def piece(ref, owner, t):
        return ref.at[pl.ds(owner * own_groups, own_groups), :, pl.ds(pl.multiple_of(t * TILE, TILE), TILE)]

    def peers():
        for dy, dx in torus_offsets(side):
            for dc in range(2):
                if (dy, dx, dc) != (0, 0, 0):
                    yield (((y + dy) % side) * side + (x + dx) % side) * 2 + (core + dc) % 2

    def send_tile(t):
        for peer in peers():
            pltpu.make_async_remote_copy(
                src_ref=piece(send, peer, t),
                dst_ref=piece(recv, me, t),
                send_sem=ssem,
                recv_sem=rsem.at[t],
                device_id={"vp": peer},
                device_id_type=MESH,
            ).start()

    def compute_tile(t):
        w_copy(t).wait()
        z = jnp.dot(hid[...], wbuf[t % SLOTS], preferred_element_type=jnp.float32)
        z = z * jnp.concatenate([invcol[...]] * (TILE // LANES), axis=1)
        top = jnp.max(z, axis=1, keepdims=True)
        e = jnp.exp(z - top)
        hi = e.astype(jnp.bfloat16)
        rest = e - hi.astype(jnp.float32)
        mid = rest.astype(jnp.bfloat16)
        low = (rest - mid.astype(jnp.float32)).astype(jnp.bfloat16)
        upto = tri[...]
        run = jnp.dot(low, upto, preferred_element_type=jnp.float32)
        run = run + jnp.dot(mid, upto, preferred_element_type=jnp.float32)
        run = run + jnp.dot(hi, upto, preferred_element_type=jnp.float32)
        at = lax.broadcasted_iota(jnp.int32, (rows, TILE), 1).astype(jnp.float32) + (t * TILE).astype(jnp.float32)
        tc = jnp.concatenate([tcol[...]] * (TILE // LANES), axis=1)
        hit = jnp.sum(jnp.where(at == tc, run, 0.0), axis=1, keepdims=True)
        lane = lax.broadcasted_iota(jnp.int32, (rows, LANES), 1)
        st = stat[...]
        st = jnp.where(lane == t, top, st)
        st = jnp.where(lane == tiles + t, run[:, TILE - 1 :], st)
        st = jnp.where(lane == 2 * tiles, st + hit, st)
        stat[...] = st
        cols = pl.ds(pl.multiple_of(t * TILE, TILE), TILE)
        for k in range(rows // SUB):
            send[k, :, cols] = run[k * SUB : (k + 1) * SUB]
        own = pl.ds(me * own_groups, own_groups)
        recv[own, :, cols] = send[own, :, cols]

    hid_copy.wait()

    def step(t, c):
        @pl.when(t + SLOTS - 1 < tiles)
        def _():
            w_copy(t + SLOTS - 1).start()

        compute_tile(t)

        @pl.when(t == 0)
        def _():
            pl.semaphore_wait(barrier, n - 1)

        @pl.when(t % 2 == 0)
        def _():
            send_tile(t // 2)

        return c

    lax.fori_loop(0, tiles, step, 0)

    lane8 = lax.broadcasted_iota(jnp.int32, (rows, LANES), 1)
    stat[...] = jnp.where(lane8 == 2 * tiles + 1, tcol[...], stat[...])
    for i in range(n):
        block = None
        for g in range(own_groups):
            k = i * own_groups + g
            part = stat[k * SUB : (k + 1) * SUB, :]
            part = part if g == 0 else pltpu.roll(part, g * width, 1)
            block = part if block is None else block + part
        stat_out[i] = block
    stat_in[me] = stat_out[me]
    for peer in peers():
        pltpu.make_async_remote_copy(
            src_ref=stat_out.at[peer], dst_ref=stat_in.at[me], send_sem=stat_ss, recv_sem=stat_rs,
            device_id={"vp": peer}, device_id_type=MESH,
        ).start()

    half = tiles // 2
    more = half + tiles // 4

    def send_more(t, c):
        send_tile(t)
        return c

    lax.fori_loop(half, more, send_more, 0)

    pltpu.make_async_copy(stat_in.at[pl.ds(0, n - 1)], stat_in.at[pl.ds(0, n - 1)], stat_rs).wait()

    lane = lax.broadcasted_iota(jnp.int32, (n, SUB, LANES), 2)
    first = lane < tiles
    values = []
    for g in range(own_groups):
        got = stat_in[...]
        if g:
            got = pltpu.roll(got, LANES - g * width, 2)
        tops = jnp.where(first, got, LOW)
        top = jnp.max(jnp.max(tops, axis=0, keepdims=True), axis=2, keepdims=True)
        weight = jnp.where(first, jnp.exp(tops - top), 0.0)
        mass = weight * jnp.where(first, pltpu.roll(got, LANES - tiles, 2), 0.0)
        upto = mass
        shift = 1
        while shift < tiles:
            upto = upto + jnp.where(lane >= shift, pltpu.roll(upto, shift, 2), 0.0)
            shift *= 2
        before = jnp.where(lane >= 1, pltpu.roll(upto, 1, 2), 0.0)
        shard = jnp.sum(mass, axis=2, keepdims=True)
        start = jnp.zeros((1, SUB, 1), jnp.float32)
        starts = []
        for s in range(n):
            starts.append(start)
            start = start + shard[s : s + 1]
        inv = 1.0 / start
        sc = weight * inv
        of = (before + jnp.concatenate(starts, axis=0)) * inv
        scale[g] = sc
        offset[g] = of
        picked = jnp.broadcast_to(got[:, :, 2 * tiles : 2 * tiles + 1], got.shape)
        target = jnp.broadcast_to(got[:, :, 2 * tiles + 1 : 2 * tiles + 2], got.shape)
        lo = (lane * TILE).astype(jnp.float32)
        hit = first & (target >= lo) & (target < lo + float(TILE))
        val = jnp.where(hit, sc * picked + of, 0.0)
        values.append(jnp.sum(jnp.sum(val, axis=0), axis=1, keepdims=True))
    lane4 = lax.broadcasted_iota(jnp.int32, (SUB, LANES), 1)
    row4 = lax.broadcasted_iota(jnp.int32, (SUB, LANES), 0)
    line = jnp.zeros((SUB, LANES), jnp.float32)
    for g in range(own_groups):
        line = jnp.where(lane4 == row4 + g * SUB, values[g], line)
    line = jnp.sum(line, axis=0, keepdims=True)
    tval[...] = line
    tall[me] = line
    for peer in peers():
        pltpu.make_async_remote_copy(
            src_ref=tval, dst_ref=tall.at[me], send_sem=t_ss, recv_sem=t_rs,
            device_id={"vp": peer}, device_id_type=MESH,
        ).start()

    lax.fori_loop(more, tiles, send_more, 0)

    for t in range(tiles):
        part = recv.at[pl.ds(0, (n - 1) * own_groups), :, pl.ds(t * TILE, TILE)]
        pltpu.make_async_copy(part, part, rsem.at[t]).wait()

        def finish(s, c):
            cols = pl.ds(pl.multiple_of(s * local_vocab + t * TILE, TILE), TILE)
            for g in range(own_groups):
                sc = scale[g, s][:, t : t + 1]
                of = offset[g, s][:, t : t + 1]
                out_ref[g * SUB : (g + 1) * SUB, cols] = recv[s * own_groups + g, :, t * TILE : (t + 1) * TILE] * sc + of
            return c

        lax.fori_loop(0, n, finish, 0, unroll=4)

    pltpu.make_async_copy(tall.at[pl.ds(0, n - 1)], tall.at[pl.ds(0, n - 1)], t_rs).wait()
    own_rows = own_groups * SUB
    lane1 = lax.broadcasted_iota(jnp.int32, (1, LANES), 1)
    acc = [jnp.zeros((1, LANES), jnp.float32) for _ in range(rows // LANES)]
    for s in range(n):
        q, off = divmod(s * own_rows, LANES)
        line = tall[s]
        line = pltpu.roll(line, off, 1) if off else line
        acc[q] = acc[q] + jnp.where(lane1 >= off, line, 0.0)
        if off + own_rows > LANES:
            acc[q + 1] = acc[q + 1] + jnp.where(lane1 < off, line, 0.0)
    for q in range(rows // LANES):
        pick_ref[:, q * LANES : (q + 1) * LANES] = acc[q]

    sent = send.at[pl.ds(0, (n - 1) * own_groups)]
    pltpu.make_async_copy(sent, sent, ssem).wait()
    pltpu.make_async_copy(stat_in.at[pl.ds(0, n - 1)], stat_in.at[pl.ds(0, n - 1)], stat_ss).wait()
    pltpu.make_async_copy(tall.at[pl.ds(0, n - 1)], tall.at[pl.ds(0, n - 1)], t_ss).wait()


def solution(mesh):
    n = mesh.shape["vp"]

    def local_step(hidden, w_local, inv_temp, target_ids):
        rows, depth = hidden.shape
        local_vocab = w_local.shape[1]
        tiles = local_vocab // TILE
        groups = rows // SUB
        own_rows = rows // n
        f32 = jnp.float32
        table, picked = pl.pallas_call(
            functools.partial(kernel, n),
            out_shape=(
                pltpu.VMEM((own_rows, n * local_vocab), f32),
                jax.ShapeDtypeStruct((1, rows), f32),
            ),
            in_specs=[
                pl.BlockSpec(memory_space=pltpu.HBM),
                pl.BlockSpec(memory_space=pltpu.HBM),
                pl.BlockSpec(memory_space=pltpu.VMEM),
                pl.BlockSpec(memory_space=pltpu.VMEM),
            ],
            out_specs=(pl.BlockSpec(memory_space=pltpu.VMEM), pl.BlockSpec(memory_space=pltpu.VMEM)),
            scratch_shapes=[
                pltpu.VMEM((rows, depth), jnp.bfloat16),
                pltpu.VMEM((SLOTS, depth, TILE), jnp.bfloat16),
                pltpu.VMEM((groups, SUB, local_vocab), f32),
                pltpu.VMEM((groups, SUB, local_vocab), f32),
                pltpu.VMEM((rows, LANES), f32),
                pltpu.VMEM((rows, LANES), f32),
                pltpu.VMEM((TILE, TILE), jnp.bfloat16),
                pltpu.VMEM((rows, LANES), f32),
                pltpu.VMEM((n, SUB, LANES), f32),
                pltpu.VMEM((n, SUB, LANES), f32),
                pltpu.VMEM((own_rows // SUB, n, SUB, LANES), f32),
                pltpu.VMEM((own_rows // SUB, n, SUB, LANES), f32),
                pltpu.VMEM((1, LANES), f32),
                pltpu.VMEM((n, 1, LANES), f32),
                pltpu.SemaphoreType.DMA,
                pltpu.SemaphoreType.DMA((SLOTS,)),
                pltpu.SemaphoreType.DMA,
                pltpu.SemaphoreType.DMA((tiles,)),
                pltpu.SemaphoreType.DMA,
                pltpu.SemaphoreType.DMA,
                pltpu.SemaphoreType.DMA,
                pltpu.SemaphoreType.DMA,
            ],
            compiler_params=pltpu.CompilerParams(collective_id=0, has_side_effects=True, vmem_limit_bytes=54 << 20),
            name="head_cdf",
        )(hidden, w_local, inv_temp.reshape(1, rows), target_ids.reshape(1, rows))
        return table, picked.reshape(rows)

    return jax.shard_map(
        local_step,
        mesh=mesh,
        in_specs=(P("dp", None), P(None, "vp"), P("dp"), P("dp")),
        out_specs=(P(("dp", "vp"), None), P("dp")),
        check_vma=False,
    )
```

time: 327 us -> 103 us (0.31)
  blocking collectives: 192 us -> 0 us
  Pallas kernels: 0 us -> 95.9 us
  local copies, waits for them, and re-layouts: 69.3 us -> 5.89 us
  matrix products: 26.5 us -> 0 us
  other arithmetic: 27.1 us -> 0.6 us
  starting transfers between devices: 10.1 us -> 0 us
    psum x1 -> x0, blocking collectives: 128 us -> none  [local_step(): cdf_at_target = lax.psum(jnp.where(in_shard, picked, 0.0), 'vp')]
    pallas_call x0 -> x1, Pallas kernels: none -> 95.9 us  [local_step(): pl.pallas_call(functools.partial(kernel, n), out_shape=(pltpu.VMEM((own_r...]
    all_gather x2 -> x0, blocking collectives: 64.2 us -> none  [the longest x1 32.3 us: local_step(): totals = lax.all_gather(local_cdf[:, -1], 'vp')]
    another operation x8 -> x0, local copies, waits for them, and re-layouts: 27.7 us -> none
    dot_general x1 -> x0, matrix products: 26.5 us -> none  [local_step(): logits = jnp.dot(hidden, w_local, preferred_element_type=jnp.float32)]
    unnamed x12 -> x3, local copies, waits for them, and re-layouts: 18.8 us -> 3.4 us
    gather x1 -> x0, local copies, waits for them, and re-layouts: 14.5 us -> none  [local_step(): jnp.take_along_axis(cdf_cols, jnp.clip(local_ids, 0, local_vocab - 1)[:,...]
    add x2 -> x0, other arithmetic: 13.9 us -> none  [local_step(): cdf_cols = local_cdf + offset[:, None]]
  transfers between devices with their start and end apart: 1 -> 0, of which waited for: 0 -> 0; matrix products, arithmetic and copies ran while one was open for 6% -> 0% of each run, Pallas kernels for 0% -> 0%
where the time goes in v1:
time: 103 us
  Pallas kernels  95.9 us (93%)
  local copies, waits for them, and re-layouts  5.89 us (6%)
    pallas_call x1, Pallas kernels, local_step(): pl.pallas_call(functools.partial(kernel, n), out_shape=(pltpu.VMEM((own_r...  95.9 us
    unnamed x3, local copies, waits for them, and re-layouts  3.4 us

profile of v1, /device:TPU:97, one launch (start us, length us, event | category | flops | bytes accessed | tf_op | source)
XLA Modules:
  0.0 103.0 jit_solution(14091148149916431075)
XLA Ops:
  0.6 1.2 %reshape.13.inv_ref = f32[1,384]{1,0:T(1,128)} reshape(f32[384]{0:T(512)} %param.6) | data formatting | bytes 3072 | tf_op jit(solution)/shard_map/reshape | solution.py:296
  1.9 1.2 %reshape.14.tgt_ref = s32[1,384]{1,0:T(1,128)} reshape(s32[384]{0:T(512)} %param.7) | data formatting | bytes 3072 | tf_op jit(solution)/shard_map/reshape | solution.py:296
  3.1 95.9 %head_cdf.1 = (f32[12,131072]{1,0:T(8,128)S(1)}, f32[1,384]{1,0:T(1,128)}) custom-call(bf16[384,5120]{1,0:T(8,128)(2,1)} %hid_hbm.1, bf16[5120,4096]{1,0:T(8,128)(2,1)} %w_hbm.1, f32[1,384]{1,0:T(1,128)} %reshape.13.inv_ref, s32[1,384]{1,0:T(1,128)} %reshape.14.tgt_ref), custom_call_target="tpu_custom_call" | custom-call | tf_op jit(solution)/shard_map/head_cdf/pallas_call | solution.py:257
  99.0 0.0 copy-start
  99.0 3.4 %copy.7 = f32[12,131072]{1,0:T(8,128)} copy(f32[12,131072]{1,0:T(8,128)S(1)} %get-tuple-element.6) | data formatting | bytes 12582912
  102.4 0.0 copy-done
  102.4 0.6 reduce
Async XLA Ops:
  99.0 3.4 %copy-start = (f32[1,384]{1,0:T(1,128)S(1)}, f32[1,384]{1,0:T(1,128)}, u32[]{:S(2)}) copy-start(f32[1,384]{1,0:T(1,128)} %get-tuple-element.5) | copy-start | bytes 4612

commit v2 on v1

v2 whole, which is shorter than its diff:
```python
import functools
import math

import jax
import jax.numpy as jnp
from jax import lax
from jax.experimental import pallas as pl
from jax.experimental.pallas import tpu as pltpu
from jax.sharding import PartitionSpec as P

MESH = pl.DeviceIdType.MESH
SUB = 4
LANES = 128
TILE = 256
PIECE = 128
SLOTS = 4
PARTS = 4
WINDOW = 5
LAG = 4
LOW = -3.0e38


def torus_offsets(side):
    def hops(d):
        return min(d, side - d)

    near = sorted(
        ((dy, dx) for dy in range(side) for dx in range(side)),
        key=lambda o: (hops(o[0]) + hops(o[1]), abs(hops(o[0]) - hops(o[1]))),
    )
    return near[1:] + near[:1]


def kernel(n, hid_hbm, w_hbm, inv_ref, tgt_ref, out_ref, pick_ref, hid, wbuf, send, recv, invcol, tcol, tri, stat,
           stat_out, stat_in, scale, offset, scale_b, offset_b, tval, tall, hsem, wsem, ssem, rsem, stat_ss, stat_rs,
           t_ss, t_rs):
    me = lax.axis_index("vp")
    rows, depth = hid.shape
    local_vocab = w_hbm.shape[1]
    tiles = local_vocab // TILE
    rounds = local_vocab // PIECE
    per = TILE // PIECE
    own_groups = rows // n // SUB
    width = 2 * tiles + 8
    side = math.isqrt(n // 2)
    core, x, y = me % 2, (me // 2) % side, me // (2 * side)
    settle = tiles + LAG

    def w_start(t):
        cols = pl.ds(pl.multiple_of(t * TILE, TILE), TILE)
        for p in range(PARTS):
            part = pl.ds(p * (depth // PARTS), depth // PARTS)
            pltpu.make_async_copy(w_hbm.at[part, cols], wbuf.at[t % SLOTS, part], wsem.at[t % SLOTS]).start()

    for p in range(PARTS):
        part = pl.ds(p * (rows // PARTS), rows // PARTS)
        pltpu.make_async_copy(hid_hbm.at[part], hid.at[part], hsem).start()
    w_start(jnp.int32(0))

    barrier = pltpu.get_barrier_semaphore()

    def knock(d, c):
        pl.semaphore_signal(barrier, inc=1, device_id={"vp": lax.rem(me + d, n)}, device_id_type=MESH)
        return c

    lax.fori_loop(1, n, knock, 0)

    eye = lax.broadcasted_iota(jnp.int32, (LANES, LANES), 0) == lax.broadcasted_iota(jnp.int32, (LANES, LANES), 1)
    shard_start = (me * local_vocab).astype(jnp.float32)
    for q in range(rows // LANES):
        cut = slice(q * LANES, (q + 1) * LANES)
        for src, dst, base in ((inv_ref, invcol, 0.0), (tgt_ref, tcol, shard_start)):
            seg = jnp.broadcast_to(src[cut].reshape(1, LANES).astype(jnp.float32), (LANES, LANES))
            col = jnp.sum(jnp.where(eye, seg, 0.0), axis=1, keepdims=True) - base
            dst[cut, :] = jnp.broadcast_to(col, (LANES, LANES))
    tri[...] = (lax.broadcasted_iota(jnp.int32, (TILE, TILE), 0) <= lax.broadcasted_iota(jnp.int32, (TILE, TILE), 1)).astype(jnp.float32).astype(jnp.bfloat16)
    stat[...] = jnp.zeros_like(stat)

    def piece(ref, owner, r):
        return ref.at[pl.ds(owner * own_groups, own_groups), :, pl.ds(pl.multiple_of(r * PIECE, PIECE), PIECE)]

    def peers():
        for dy, dx in torus_offsets(side):
            for dc in range(2):
                if (dy, dx, dc) != (0, 0, 0):
                    yield (((y + dy) % side) * side + (x + dx) % side) * 2 + (core + dc) % 2

    def send_round(r):
        for peer in peers():
            pltpu.make_async_remote_copy(
                src_ref=piece(send, peer, r),
                dst_ref=piece(recv, me, r),
                send_sem=ssem.at[r],
                recv_sem=rsem.at[r],
                device_id={"vp": peer},
                device_id_type=MESH,
            ).start()

    def sent_round(r):
        part = send.at[pl.ds(0, (n - 1) * own_groups), :, pl.ds(0, PIECE)]
        pltpu.make_async_copy(part, part, ssem.at[r]).wait()

    def compute_tile(t):
        pltpu.make_async_copy(wbuf.at[t % SLOTS], wbuf.at[t % SLOTS], wsem.at[t % SLOTS]).wait()

        @pl.when(t == 0)
        def _():
            w_start(t + 1)

        @pl.when(t + 2 < tiles)
        def _():
            w_start(t + 2)

        z = jnp.dot(hid[...], wbuf[t % SLOTS], preferred_element_type=jnp.float32)
        z = z * jnp.concatenate([invcol[...]] * (TILE // LANES), axis=1)
        top = jnp.max(z, axis=1, keepdims=True)
        e = jnp.exp(z - top)
        hi = e.astype(jnp.bfloat16)
        rest = e - hi.astype(jnp.float32)
        mid = rest.astype(jnp.bfloat16)
        low = (rest - mid.astype(jnp.float32)).astype(jnp.bfloat16)
        upto = tri[...]
        run = jnp.dot(low, upto, preferred_element_type=jnp.float32)
        run = run + jnp.dot(mid, upto, preferred_element_type=jnp.float32)
        run = run + jnp.dot(hi, upto, preferred_element_type=jnp.float32)
        cols = pl.ds(pl.multiple_of(t * TILE, TILE), TILE)
        for k in range(rows // SUB):
            send[k, :, cols] = run[k * SUB : (k + 1) * SUB]
        at = lax.broadcasted_iota(jnp.int32, (rows, TILE), 1).astype(jnp.float32) + (t * TILE).astype(jnp.float32)
        tc = jnp.concatenate([tcol[...]] * (TILE // LANES), axis=1)
        hit = jnp.sum(jnp.where(at == tc, run, 0.0), axis=1, keepdims=True)
        lane = lax.broadcasted_iota(jnp.int32, (rows, LANES), 1)
        st = stat[...]
        st = jnp.where(lane == t, top, st)
        st = jnp.where(lane == tiles + t, run[:, TILE - 1 :], st)
        st = jnp.where(lane == 2 * tiles, st + hit, st)
        stat[...] = st
        own = pl.ds(me * own_groups, own_groups)
        recv[own, :, cols] = send[own, :, cols]

    def send_statistics():
        lane8 = lax.broadcasted_iota(jnp.int32, (rows, LANES), 1)
        stat[...] = jnp.where(lane8 == 2 * tiles + 1, tcol[...], stat[...])
        for i in range(n):
            block = None
            for g in range(own_groups):
                k = i * own_groups + g
                part = stat[k * SUB : (k + 1) * SUB, :]
                part = part if g == 0 else pltpu.roll(part, g * width, 1)
                block = part if block is None else block + part
            stat_out[i] = block
        stat_in[me] = stat_out[me]

        def go(d, c):
            peer = lax.rem(me + d, n)
            pltpu.make_async_remote_copy(
                src_ref=stat_out.at[peer], dst_ref=stat_in.at[me], send_sem=stat_ss, recv_sem=stat_rs,
                device_id={"vp": peer}, device_id_type=MESH,
            ).start()
            return c

        lax.fori_loop(1, n, go, 0)

    def take_statistics():
        pltpu.make_async_copy(stat_in.at[pl.ds(0, n - 1)], stat_in.at[pl.ds(0, n - 1)], stat_rs).wait()
        lane = lax.broadcasted_iota(jnp.int32, (n, SUB, LANES), 2)
        first = lane < tiles
        lane4 = lax.broadcasted_iota(jnp.int32, (SUB, LANES), 1)
        row4 = lax.broadcasted_iota(jnp.int32, (SUB, LANES), 0)
        line = jnp.zeros((SUB, LANES), jnp.float32)
        for g in range(own_groups):
            got = stat_in[...]
            if g:
                got = pltpu.roll(got, LANES - g * width, 2)
            tops = jnp.where(first, got, LOW)
            top = jnp.max(jnp.max(tops, axis=0, keepdims=True), axis=2, keepdims=True)
            weight = jnp.where(first, jnp.exp(tops - top), 0.0)
            mass = weight * jnp.where(first, pltpu.roll(got, LANES - tiles, 2), 0.0)
            upto = mass
            shift = 1
            while shift < tiles:
                upto = upto + jnp.where(lane >= shift, pltpu.roll(upto, shift, 2), 0.0)
                shift *= 2
            before = jnp.where(lane >= 1, pltpu.roll(upto, 1, 2), 0.0)
            shard = jnp.sum(mass, axis=2, keepdims=True)
            start = jnp.zeros((1, SUB, 1), jnp.float32)
            starts = []
            for s in range(n):
                starts.append(start)
                start = start + shard[s : s + 1]
            inv = 1.0 / start
            sc = weight * inv
            of = (before + jnp.concatenate(starts, axis=0)) * inv
            scale[g] = sc
            offset[g] = of
            picked = jnp.broadcast_to(got[:, :, 2 * tiles : 2 * tiles + 1], got.shape)
            target = jnp.broadcast_to(got[:, :, 2 * tiles + 1 : 2 * tiles + 2], got.shape)
            lo = (lane * TILE).astype(jnp.float32)
            hit = first & (target >= lo) & (target < lo + float(TILE))
            val = jnp.where(hit, sc * picked + of, 0.0)
            val = jnp.sum(jnp.sum(val, axis=0), axis=1, keepdims=True)
            line = jnp.where(lane4 == row4 + g * SUB, val, line)
        line = jnp.sum(line, axis=0, keepdims=True)
        tval[...] = line
        tall[me] = line

        def go(d, c):
            pltpu.make_async_remote_copy(
                src_ref=tval, dst_ref=tall.at[me], send_sem=t_ss, recv_sem=t_rs,
                device_id={"vp": lax.rem(me + d, n)}, device_id_type=MESH,
            ).start()
            return c

        lax.fori_loop(1, n, go, 0)

        def spread(t, c):
            for g in range(own_groups):
                for ref, wide in ((scale, scale_b), (offset, offset_b)):
                    v = ref[g]
                    wide[t, g] = jnp.broadcast_to(v[:, :, :1], v.shape)
                    ref[g] = pltpu.roll(v, LANES - 1, 2)
            return c

        lax.fori_loop(0, tiles, spread, 0)

    def finish_round(r):
        part = recv.at[pl.ds(0, (n - 1) * own_groups), :, pl.ds(0, PIECE)]
        pltpu.make_async_copy(part, part, rsem.at[r]).wait()
        t = r // per
        here = pl.ds(pl.multiple_of(r * PIECE, PIECE), PIECE)

        def one(s, c):
            cols = pl.ds(pl.multiple_of(s * local_vocab + r * PIECE, PIECE), PIECE)
            for g in range(own_groups):
                out_ref[g * SUB : (g + 1) * SUB, cols] = recv[s * own_groups + g, :, here] * scale_b[t, g, s] + offset_b[t, g, s]
            return c

        lax.fori_loop(0, n, one, 0, unroll=8)

    pltpu.make_async_copy(hid, hid, hsem).wait()

    def step(r, c):
        @pl.when(r < tiles)
        def _():
            compute_tile(r)

        @pl.when(r == 0)
        def _():
            pl.semaphore_wait(barrier, n - 1)

        @pl.when(r == tiles)
        def _():
            send_statistics()

        @pl.when(r == settle)
        def _():
            take_statistics()

        @pl.when(r >= WINDOW)
        def _():
            sent_round(r - WINDOW)

        send_round(r)

        @pl.when(r >= settle)
        def _():
            finish_round((r - settle) * 2)
            finish_round((r - settle) * 2 + 1)

        return c

    lax.fori_loop(0, rounds, step, 0)

    pltpu.make_async_copy(tall.at[pl.ds(0, n - 1)], tall.at[pl.ds(0, n - 1)], t_rs).wait()
    own_rows = own_groups * SUB
    lane1 = lax.broadcasted_iota(jnp.int32, (1, LANES), 1)
    acc = [jnp.zeros((1, LANES), jnp.float32) for _ in range(rows // LANES)]
    for s in range(n):
        q, off = divmod(s * own_rows, LANES)
        line = tall[s]
        line = pltpu.roll(line, off, 1) if off else line
        acc[q] = acc[q] + jnp.where(lane1 >= off, line, 0.0)
        if off + own_rows > LANES:
            acc[q + 1] = acc[q + 1] + jnp.where(lane1 < off, line, 0.0)
    for q in range(rows // LANES):
        pick_ref[q * LANES : (q + 1) * LANES] = acc[q].reshape(LANES)

    def last(r, c):
        finish_round(r)
        return c

    lax.fori_loop((rounds - settle) * 2, rounds, last, 0)

    def left(r, c):
        sent_round(r)
        return c

    lax.fori_loop(rounds - WINDOW, rounds, left, 0)
    pltpu.make_async_copy(stat_in.at[pl.ds(0, n - 1)], stat_in.at[pl.ds(0, n - 1)], stat_ss).wait()
    pltpu.make_async_copy(tall.at[pl.ds(0, n - 1)], tall.at[pl.ds(0, n - 1)], t_ss).wait()


def solution(mesh):
    n = mesh.shape["vp"]

    def local_step(hidden, w_local, inv_temp, target_ids):
        rows, depth = hidden.shape
        local_vocab = w_local.shape[1]
        tiles = local_vocab // TILE
        groups = rows // SUB
        own_rows = rows // n
        f32 = jnp.float32
        table, picked = pl.pallas_call(
            functools.partial(kernel, n),
            out_shape=(
                pltpu.VMEM((own_rows, n * local_vocab), f32),
                jax.ShapeDtypeStruct((rows,), f32),
            ),
            in_specs=[
                pl.BlockSpec(memory_space=pltpu.HBM),
                pl.BlockSpec(memory_space=pltpu.HBM),
                pl.BlockSpec(memory_space=pltpu.VMEM),
                pl.BlockSpec(memory_space=pltpu.VMEM),
            ],
            out_specs=(pl.BlockSpec(memory_space=pltpu.VMEM), pl.BlockSpec(memory_space=pltpu.VMEM)),
            scratch_shapes=[
                pltpu.VMEM((rows, depth), jnp.bfloat16),
                pltpu.VMEM((SLOTS, depth, TILE), jnp.bfloat16),
                pltpu.VMEM((groups, SUB, local_vocab), f32),
                pltpu.VMEM((groups, SUB, local_vocab), f32),
                pltpu.VMEM((rows, LANES), f32),
                pltpu.VMEM((rows, LANES), f32),
                pltpu.VMEM((TILE, TILE), jnp.bfloat16),
                pltpu.VMEM((rows, LANES), f32),
                pltpu.VMEM((n, SUB, LANES), f32),
                pltpu.VMEM((n, SUB, LANES), f32),
                pltpu.VMEM((own_rows // SUB, n, SUB, LANES), f32),
                pltpu.VMEM((own_rows // SUB, n, SUB, LANES), f32),
                pltpu.VMEM((tiles, own_rows // SUB, n, SUB, LANES), f32),
                pltpu.VMEM((tiles, own_rows // SUB, n, SUB, LANES), f32),
                pltpu.VMEM((1, LANES), f32),
                pltpu.VMEM((n, 1, LANES), f32),
                pltpu.SemaphoreType.DMA,
                pltpu.SemaphoreType.DMA((SLOTS,)),
                pltpu.SemaphoreType.DMA((local_vocab // PIECE,)),
                pltpu.SemaphoreType.DMA((local_vocab // PIECE,)),
                pltpu.SemaphoreType.DMA,
                pltpu.SemaphoreType.DMA,
                pltpu.SemaphoreType.DMA,
                pltpu.SemaphoreType.DMA,
            ],
            compiler_params=pltpu.CompilerParams(collective_id=0, has_side_effects=True, vmem_limit_bytes=54 << 20),
            name="head_cdf",
        )(hidden, w_local, inv_temp, target_ids)
        return table, picked

    return jax.shard_map(
        local_step,
        mesh=mesh,
        in_specs=(P("dp", None), P(None, "vp"), P("dp"), P("dp")),
        out_specs=(P(("dp", "vp"), None), P("dp")),
        check_vma=False,
    )
```

time: 103 us -> 110 us (1.068)
  Pallas kernels: 95.9 us -> 105 us
  local copies, waits for them, and re-layouts: 5.89 us -> 3.98 us
    pallas_call x1, Pallas kernels: 95.9 us -> 105 us  [local_step(): pl.pallas_call(functools.partial(kernel, n), out_shape=(pltpu.VMEM((own_r...]
    reshape x2 -> x0, local copies, waits for them, and re-layouts: 2.49 us -> none  [the longest x1 1.25 us: local_step(): inv_temp.reshape(1, rows)]
    unnamed x3 -> x4, local copies, waits for them, and re-layouts: 3.4 us -> 3.98 us
where the time goes in v2:
time: 110 us; the launch traced here: 109 us
  Pallas kernels  105 us (95%)
  local copies, waits for them, and re-layouts  3.98 us (4%)
    pallas_call x1, Pallas kernels, local_step(): pl.pallas_call(functools.partial(kernel, n), out_shape=(pltpu.VMEM((own_r...  105 us
    unnamed x4, local copies, waits for them, and re-layouts  3.98 us

profile of v2, /device:TPU:97, one launch (start us, length us, event | category | flops | bytes accessed | tf_op | source)
XLA Modules:
  0.0 109.4 jit_solution(6114776061821893269)
XLA Ops:
  0.6 104.8 %head_cdf.1 = (f32[12,131072]{1,0:T(8,128)S(1)}, f32[384]{0:T(512)}) custom-call(bf16[384,5120]{1,0:T(8,128)(2,1)} %hid_hbm.1, bf16[5120,4096]{1,0:T(8,128)(2,1)} %w_hbm.1, f32[384]{0:T(512)} %inv_ref.1, s32[384]{0:T(512)} %tgt_ref.1), custom_call_target="tpu_custom_call" | custom-call | tf_op jit(solution)/shard_map/head_cdf/pallas_call | solution.py:313
  105.4 0.0 copy-start
  105.4 3.4 %copy.8 = f32[12,131072]{1,0:T(8,128)} copy(f32[12,131072]{1,0:T(8,128)S(1)} %get-tuple-element.2) | data formatting | bytes 12582912
  108.8 0.0 copy-done
  108.8 0.6 copy.9
Async XLA Ops:
  105.4 3.4 %copy-start = (f32[384]{0:T(512)S(1)}, f32[384]{0:T(512)}, u32[]{:S(2)}) copy-start(f32[384]{0:T(512)} %get-tuple-element.7) | copy-start | bytes 4612

commit v3 on v2

--- a/solution.py
+++ b/solution.py
@@ -12,39 +12,31 @@
 SUB = 4
 LANES = 128
 TILE = 256
-PIECE = 128
-SLOTS = 4
+SLOTS = 3
 PARTS = 4
-WINDOW = 5
-LAG = 4
 LOW = -3.0e38
 
 
-def torus_offsets(side):
-    def hops(d):
-        return min(d, side - d)
-
-    near = sorted(
-        ((dy, dx) for dy in range(side) for dx in range(side)),
-        key=lambda o: (hops(o[0]) + hops(o[1]), abs(hops(o[0]) - hops(o[1]))),
-    )
-    return near[1:] + near[:1]
-
-
-def kernel(n, hid_hbm, w_hbm, inv_ref, tgt_ref, out_ref, pick_ref, hid, wbuf, send, recv, invcol, tcol, tri, stat,
-           stat_out, stat_in, scale, offset, scale_b, offset_b, tval, tall, hsem, wsem, ssem, rsem, stat_ss, stat_rs,
-           t_ss, t_rs):
+def kernel(n, hid_hbm, w_hbm, inv_ref, tgt_ref, out_ref, pick_ref, hid, wbuf, send, mid, recv, invcol, tcol, tri, stat,
+           stat_out, stat_in, scale, offset, scale_b, offset_b, tval, tall, hsem, wsem, one_ss, one_rs, two_ss, two_rs,
+           stat_ss, stat_rs, t_ss, t_rs):
     me = lax.axis_index("vp")
     rows, depth = hid.shape
     local_vocab = w_hbm.shape[1]
     tiles = local_vocab // TILE
-    rounds = local_vocab // PIECE
-    per = TILE // PIECE
     own_groups = rows // n // SUB
     width = 2 * tiles + 8
     side = math.isqrt(n // 2)
     core, x, y = me % 2, (me // 2) % side, me // (2 * side)
-    settle = tiles + LAG
+    a = x + core * (y - x)
+    b = y + core * (x - y)
+
+    def device(a_, b_, core_):
+        row = b_ + core * (a_ - b_)
+        col = a_ + core * (b_ - a_)
+        return {"vp": (row * side + col) * 2 + core_}
+
+    slab = 2 * side * own_groups
 
     def w_start(t):
         cols = pl.ds(pl.multiple_of(t * TILE, TILE), TILE)
@@ -76,29 +68,40 @@
     tri[...] = (lax.broadcasted_iota(jnp.int32, (TILE, TILE), 0) <= lax.broadcasted_iota(jnp.int32, (TILE, TILE), 1)).astype(jnp.float32).astype(jnp.bfloat16)
     stat[...] = jnp.zeros_like(stat)
 
-    def piece(ref, owner, r):
-        return ref.at[pl.ds(owner * own_groups, own_groups), :, pl.ds(pl.multiple_of(r * PIECE, PIECE), PIECE)]
-
-    def peers():
-        for dy, dx in torus_offsets(side):
-            for dc in range(2):
-                if (dy, dx, dc) != (0, 0, 0):
-                    yield (((y + dy) % side) * side + (x + dx) % side) * 2 + (core + dc) % 2
-
-    def send_round(r):
-        for peer in peers():
+    def columns(t):
+        return pl.ds(pl.multiple_of(t * TILE, TILE), TILE)
+
+    def first_leg(r):
+        for hop in (1, side - 1, *range(2, side - 1)):
+            to = (a + hop) % side
             pltpu.make_async_remote_copy(
-                src_ref=piece(send, peer, r),
-                dst_ref=piece(recv, me, r),
-                send_sem=ssem.at[r],
-                recv_sem=rsem.at[r],
-                device_id={"vp": peer},
+                src_ref=send.at[pl.ds(to * slab, slab), :, columns(r)],
+                dst_ref=mid.at[a, :, :, columns(r)],
+                send_sem=one_ss,
+                recv_sem=one_rs.at[r],
+                device_id=device(to, b, core),
                 device_id_type=MESH,
             ).start()
 
-    def sent_round(r):
-        part = send.at[pl.ds(0, (n - 1) * own_groups), :, pl.ds(0, PIECE)]
-        pltpu.make_async_copy(part, part, ssem.at[r]).wait()
+    def second_leg(r):
+        part = mid.at[pl.ds(0, side - 1), :, :, pl.ds(0, TILE)]
+        pltpu.make_async_copy(part, part, one_rs.at[r]).wait()
+
+        def onward(to, core_):
+            pltpu.make_async_remote_copy(
+                src_ref=mid.at[:, pl.ds((to * 2 + core_) * own_groups, own_groups), :, columns(r)],
+                dst_ref=recv.at[core * side + b, :, :, :, columns(r)],
+                send_sem=two_ss,
+                recv_sem=two_rs.at[r],
+                device_id=device(a, to, core_),
+                device_id_type=MESH,
+            ).start()
+
+        for hop in (1, side - 1, *range(2, side - 1)):
+            for core_ in range(2):
+                onward((b + hop) % side, core_)
+        onward(b, 1 - core)
+        recv[core * side + b, :, :, :, columns(r)] = mid[:, pl.ds((b * 2 + core) * own_groups, own_groups), :, columns(r)]
 
     def compute_tile(t):
         pltpu.make_async_copy(wbuf.at[t % SLOTS], wbuf.at[t % SLOTS], wsem.at[t % SLOTS]).wait()
@@ -117,15 +120,18 @@
         e = jnp.exp(z - top)
         hi = e.astype(jnp.bfloat16)
         rest = e - hi.astype(jnp.float32)
-        mid = rest.astype(jnp.bfloat16)
-        low = (rest - mid.astype(jnp.float32)).astype(jnp.bfloat16)
+        more = rest.astype(jnp.bfloat16)
+        low = (rest - more.astype(jnp.float32)).astype(jnp.bfloat16)
         upto = tri[...]
         run = jnp.dot(low, upto, preferred_element_type=jnp.float32)
-        run = run + jnp.dot(mid, upto, preferred_element_type=jnp.float32)
+        run = run + jnp.dot(more, upto, preferred_element_type=jnp.float32)
         run = run + jnp.dot(hi, upto, preferred_element_type=jnp.float32)
-        cols = pl.ds(pl.multiple_of(t * TILE, TILE), TILE)
+        cols = columns(t)
         for k in range(rows // SUB):
-            send[k, :, cols] = run[k * SUB : (k + 1) * SUB]
+            owner, g = divmod(k, own_groups)
+            oy, ox, oc = owner // (2 * side), (owner // 2) % side, owner % 2
+            x_first, y_first = ((ox * side + oy) * 2 + oc) * own_groups + g, ((oy * side + ox) * 2 + oc) * own_groups + g
+            send[x_first + core * (y_first - x_first), :, cols] = run[k * SUB : (k + 1) * SUB]
         at = lax.broadcasted_iota(jnp.int32, (rows, TILE), 1).astype(jnp.float32) + (t * TILE).astype(jnp.float32)
         tc = jnp.concatenate([tcol[...]] * (TILE // LANES), axis=1)
         hit = jnp.sum(jnp.where(at == tc, run, 0.0), axis=1, keepdims=True)
@@ -135,8 +141,7 @@
         st = jnp.where(lane == tiles + t, run[:, TILE - 1 :], st)
         st = jnp.where(lane == 2 * tiles, st + hit, st)
         stat[...] = st
-        own = pl.ds(me * own_groups, own_groups)
-        recv[own, :, cols] = send[own, :, cols]
+        mid[a, :, :, cols] = send[pl.ds(a * slab, slab), :, cols]
 
     def send_statistics():
         lane8 = lax.broadcasted_iota(jnp.int32, (rows, LANES), 1)
@@ -224,52 +229,75 @@
         lax.fori_loop(0, tiles, spread, 0)
 
     def finish_round(r):
-        part = recv.at[pl.ds(0, (n - 1) * own_groups), :, pl.ds(0, PIECE)]
-        pltpu.make_async_copy(part, part, rsem.at[r]).wait()
-        t = r // per
-        here = pl.ds(pl.multiple_of(r * PIECE, PIECE), PIECE)
-
-        def one(s, c):
-            cols = pl.ds(pl.multiple_of(s * local_vocab + r * PIECE, PIECE), PIECE)
+        part = recv.at[pl.ds(0, 2 * side - 1), :, :, :, pl.ds(0, TILE)]
+        pltpu.make_async_copy(part, part, two_rs.at[r]).wait()
+
+        def one(q, c):
+            relay, u = q // side, q % side
+            core_, v = relay // side, relay % side
+            row = v + core_ * (u - v)
+            col = u + core_ * (v - u)
+            s = (row * side + col) * 2 + core_
             for g in range(own_groups):
-                out_ref[g * SUB : (g + 1) * SUB, cols] = recv[s * own_groups + g, :, here] * scale_b[t, g, s] + offset_b[t, g, s]
+                sc, of = scale_b[r, g, s], offset_b[r, g, s]
+                for h in range(TILE // LANES):
+                    here = pl.ds(pl.multiple_of(r * TILE + h * LANES, LANES), LANES)
+                    cols = pl.ds(pl.multiple_of(s * local_vocab + r * TILE + h * LANES, LANES), LANES)
+                    out_ref[g * SUB : (g + 1) * SUB, cols] = recv[relay, u, g, :, here] * sc + of
             return c
 
-        lax.fori_loop(0, n, one, 0, unroll=8)
+        lax.fori_loop(0, n, one, 0, unroll=4)
 
     pltpu.make_async_copy(hid, hid, hsem).wait()
 
-    def step(r, c):
-        @pl.when(r < tiles)
-        def _():
-            compute_tile(r)
-
-        @pl.when(r == 0)
+    def early(t, c):
+        compute_tile(t)
+
+        @pl.when(t == 0)
         def _():
             pl.semaphore_wait(barrier, n - 1)
-
-        @pl.when(r == tiles)
-        def _():
-            send_statistics()
-
-        @pl.when(r == settle)
+            first_leg(t)
+
+        @pl.when(t == 1)
+        def _():
+            first_leg(t)
+
+        @pl.when((t >= 2) & (t % 2 == 0))
+        def _():
+            first_leg(t // 2 + 1)
+
+        @pl.when((t >= 3) & (t % 2 == 1))
+        def _():
+            second_leg((t - 3) // 2)
+
+        return c
+
+    lax.fori_loop(0, tiles, early, 0)
+    gone = tiles // 2 + 1
+    send_statistics()
+
+    take_at = gone + 3
+
+    def late(k, c):
+        first_leg(k)
+
+        @pl.when(k == take_at)
         def _():
             take_statistics()
 
-        @pl.when(r >= WINDOW)
-        def _():
-            sent_round(r - WINDOW)
-
-        send_round(r)
-
-        @pl.when(r >= settle)
-        def _():
-            finish_round((r - settle) * 2)
-            finish_round((r - settle) * 2 + 1)
+        second_leg(k - 2)
+
+        @pl.when(k >= take_at)
+        def _():
+            for m in range(3):
+                finish_round((k - take_at) * 3 + m)
 
         return c
 
-    lax.fori_loop(0, rounds, step, 0)
+    lax.fori_loop(gone, tiles, late, 0)
+    done = (tiles - take_at) * 3
+    second_leg(tiles - 2)
+    second_leg(tiles - 1)
 
     pltpu.make_async_copy(tall.at[pl.ds(0, n - 1)], tall.at[pl.ds(0, n - 1)], t_rs).wait()
     own_rows = own_groups * SUB
@@ -289,19 +317,17 @@
         finish_round(r)
         return c
 
-    lax.fori_loop((rounds - settle) * 2, rounds, last, 0)
-
-    def left(r, c):
-        sent_round(r)
-        return c
-
-    lax.fori_loop(rounds - WINDOW, rounds, left, 0)
+    lax.fori_loop(done, tiles, last, 0)
+
+    pltpu.make_async_copy(mid.at[pl.ds(0, side - 1)], mid.at[pl.ds(0, side - 1)], one_ss).wait()
+    pltpu.make_async_copy(recv.at[pl.ds(0, 2 * side - 1)], recv.at[pl.ds(0, 2 * side - 1)], two_ss).wait()
     pltpu.make_async_copy(stat_in.at[pl.ds(0, n - 1)], stat_in.at[pl.ds(0, n - 1)], stat_ss).wait()
     pltpu.make_async_copy(tall.at[pl.ds(0, n - 1)], tall.at[pl.ds(0, n - 1)], t_ss).wait()
 
 
 def solution(mesh):
     n = mesh.shape["vp"]
+    side = math.isqrt(n // 2)
 
     def local_step(hidden, w_local, inv_temp, target_ids):
         rows, depth = hidden.shape
@@ -327,7 +353,8 @@
                 pltpu.VMEM((rows, depth), jnp.bfloat16),
                 pltpu.VMEM((SLOTS, depth, TILE), jnp.bfloat16),
                 pltpu.VMEM((groups, SUB, local_vocab), f32),
-                pltpu.VMEM((groups, SUB, local_vocab), f32),
+                pltpu.VMEM((side, groups // side, SUB, local_vocab), f32),
+                pltpu.VMEM((2 * side, side, own_rows // SUB, SUB, local_vocab), f32),
                 pltpu.VMEM((rows, LANES), f32),
                 pltpu.VMEM((rows, LANES), f32),
                 pltpu.VMEM((TILE, TILE), jnp.bfloat16),
@@ -342,8 +369,10 @@
                 pltpu.VMEM((n, 1, LANES), f32),
                 pltpu.SemaphoreType.DMA,
                 pltpu.SemaphoreType.DMA((SLOTS,)),
-                pltpu.SemaphoreType.DMA((local_vocab // PIECE,)),
-                pltpu.SemaphoreType.DMA((local_vocab // PIECE,)),
+                pltpu.SemaphoreType.DMA,
+                pltpu.SemaphoreType.DMA((tiles,)),
+                pltpu.SemaphoreType.DMA,
+                pltpu.SemaphoreType.DMA((tiles,)),
                 pltpu.SemaphoreType.DMA,
                 pltpu.SemaphoreType.DMA,
                 pltpu.SemaphoreType.DMA,

time: 110 us -> 97.6 us (0.89)
  Pallas kernels: 105 us -> 92.8 us
    pallas_call x1, Pallas kernels: 105 us -> 92.8 us  [local_step(): pl.pallas_call(functools.partial(kernel, n), out_shape=(pltpu.VMEM((own_r...]
where the time goes in v3:
time: 97.6 us; the launch traced here: 97.5 us
  Pallas kernels  92.8 us (95%)
  local copies, waits for them, and re-layouts  3.98 us (4%)
    pallas_call x1, Pallas kernels, local_step(): pl.pallas_call(functools.partial(kernel, n), out_shape=(pltpu.VMEM((own_r...  92.8 us
    unnamed x4, local copies, waits for them, and re-layouts  3.98 us

profile of v3, /device:TPU:97, one launch (start us, length us, event | category | flops | bytes accessed | tf_op | source)
XLA Modules:
  0.0 97.5 jit_solution(9789692139508561169)
XLA Ops:
  0.6 92.8 %head_cdf.1 = (f32[12,131072]{1,0:T(8,128)S(1)}, f32[384]{0:T(512)}) custom-call(bf16[384,5120]{1,0:T(8,128)(2,1)} %hid_hbm.1, bf16[5120,4096]{1,0:T(8,128)(2,1)} %w_hbm.1, f32[384]{0:T(512)} %inv_ref.1, s32[384]{0:T(512)} %tgt_ref.1), custom_call_target="tpu_custom_call" | custom-call | tf_op jit(solution)/shard_map/head_cdf/pallas_call | solution.py:339
  93.5 0.0 copy-start
  93.5 3.4 %copy.8 = f32[12,131072]{1,0:T(8,128)} copy(f32[12,131072]{1,0:T(8,128)S(1)} %get-tuple-element.2) | data formatting | bytes 12582912
  96.9 0.0 copy-done
  96.9 0.6 copy.9
Async XLA Ops:
  93.5 3.4 %copy-start = (f32[384]{0:T(512)S(1)}, f32[384]{0:T(512)}, u32[]{:S(2)}) copy-start(f32[384]{0:T(512)} %get-tuple-element.7) | copy-start | bytes 4612

commit v4 on v3

--- a/solution.py
+++ b/solution.py
@@ -12,8 +12,10 @@
 SUB = 4
 LANES = 128
 TILE = 256
+HALF = TILE // 2
 SLOTS = 3
 PARTS = 4
+STORES = 8
 LOW = -3.0e38
 
 
@@ -71,28 +73,36 @@
     def columns(t):
         return pl.ds(pl.multiple_of(t * TILE, TILE), TILE)
 
-    def first_leg(r):
+    def round_columns(r, part):
+        if part is None:
+            return columns(r), r
+        start = (tiles - 1) * TILE + part * HALF
+        return pl.ds(start, HALF), tiles - 1 + part
+
+    def first_leg(r, half=None):
+        cols, k = round_columns(r, half)
         for hop in (1, side - 1, *range(2, side - 1)):
             to = (a + hop) % side
             pltpu.make_async_remote_copy(
-                src_ref=send.at[pl.ds(to * slab, slab), :, columns(r)],
-                dst_ref=mid.at[a, :, :, columns(r)],
+                src_ref=send.at[pl.ds(to * slab, slab), :, cols],
+                dst_ref=mid.at[a, :, :, cols],
                 send_sem=one_ss,
-                recv_sem=one_rs.at[r],
+                recv_sem=one_rs.at[k],
                 device_id=device(to, b, core),
                 device_id_type=MESH,
             ).start()
 
-    def second_leg(r):
-        part = mid.at[pl.ds(0, side - 1), :, :, pl.ds(0, TILE)]
-        pltpu.make_async_copy(part, part, one_rs.at[r]).wait()
+    def second_leg(r, half=None):
+        cols, k = round_columns(r, half)
+        part = mid.at[pl.ds(0, side - 1), :, :, pl.ds(0, TILE if half is None else HALF)]
+        pltpu.make_async_copy(part, part, one_rs.at[k]).wait()
 
         def onward(to, core_):
             pltpu.make_async_remote_copy(
-                src_ref=mid.at[:, pl.ds((to * 2 + core_) * own_groups, own_groups), :, columns(r)],
-                dst_ref=recv.at[core * side + b, :, :, :, columns(r)],
+                src_ref=mid.at[:, pl.ds((to * 2 + core_) * own_groups, own_groups), :, cols],
+                dst_ref=recv.at[core * side + b, :, :, :, cols],
                 send_sem=two_ss,
-                recv_sem=two_rs.at[r],
+                recv_sem=two_rs.at[k],
                 device_id=device(a, to, core_),
                 device_id_type=MESH,
             ).start()
@@ -101,7 +111,7 @@
             for core_ in range(2):
                 onward((b + hop) % side, core_)
         onward(b, 1 - core)
-        recv[core * side + b, :, :, :, columns(r)] = mid[:, pl.ds((b * 2 + core) * own_groups, own_groups), :, columns(r)]
+        recv[core * side + b, :, :, :, cols] = mid[:, pl.ds((b * 2 + core) * own_groups, own_groups), :, cols]
 
     def compute_tile(t):
         pltpu.make_async_copy(wbuf.at[t % SLOTS], wbuf.at[t % SLOTS], wsem.at[t % SLOTS]).wait()
@@ -218,19 +228,20 @@
 
         lax.fori_loop(1, n, go, 0)
 
-        def spread(t, c):
-            for g in range(own_groups):
-                for ref, wide in ((scale, scale_b), (offset, offset_b)):
-                    v = ref[g]
-                    wide[t, g] = jnp.broadcast_to(v[:, :, :1], v.shape)
-                    ref[g] = pltpu.roll(v, LANES - 1, 2)
-            return c
-
-        lax.fori_loop(0, tiles, spread, 0)
-
-    def finish_round(r):
-        part = recv.at[pl.ds(0, 2 * side - 1), :, :, :, pl.ds(0, TILE)]
-        pltpu.make_async_copy(part, part, two_rs.at[r]).wait()
+    def widen(t):
+        for g in range(own_groups):
+            for ref, wide in ((scale, scale_b), (offset, offset_b)):
+                v = ref[g]
+                wide[g] = jnp.broadcast_to(v[:, :, :1], v.shape)
+                ref[g] = pltpu.roll(v, LANES - 1, 2)
+
+    def finish_round(r, half=None):
+        size = TILE if half is None else HALF
+        base = r * TILE if half is None else (tiles - 1) * TILE + half * HALF
+        if not half:
+            widen(r)
+        part = recv.at[pl.ds(0, 2 * side - 1), :, :, :, pl.ds(0, size)]
+        pltpu.make_async_copy(part, part, two_rs.at[r if half is None else tiles - 1 + half]).wait()
 
         def one(q, c):
             relay, u = q // side, q % side
@@ -239,10 +250,10 @@
             col = u + core_ * (v - u)
             s = (row * side + col) * 2 + core_
             for g in range(own_groups):
-                sc, of = scale_b[r, g, s], offset_b[r, g, s]
-                for h in range(TILE // LANES):
-                    here = pl.ds(pl.multiple_of(r * TILE + h * LANES, LANES), LANES)
-                    cols = pl.ds(pl.multiple_of(s * local_vocab + r * TILE + h * LANES, LANES), LANES)
+                sc, of = scale_b[g, s], offset_b[g, s]
+                for h in range(size // LANES):
+                    here = pl.ds(pl.multiple_of(base + h * LANES, LANES), LANES)
+                    cols = pl.ds(pl.multiple_of(s * local_vocab + base + h * LANES, LANES), LANES)
                     out_ref[g * SUB : (g + 1) * SUB, cols] = recv[relay, u, g, :, here] * sc + of
             return c
 
@@ -273,19 +284,21 @@
         return c
 
     lax.fori_loop(0, tiles, early, 0)
-    gone = tiles // 2 + 1
     send_statistics()
 
-    take_at = gone + 3
+    next_one, next_two = tiles // 2 + 1, tiles // 2 - 1
+    first_leg(jnp.int32(next_one))
+    lead = next_one + 1 - next_two
+    take_at = next_two + 3
 
     def late(k, c):
-        first_leg(k)
+        first_leg(k + lead)
 
         @pl.when(k == take_at)
         def _():
             take_statistics()
 
-        second_leg(k - 2)
+        second_leg(k)
 
         @pl.when(k >= take_at)
         def _():
@@ -294,11 +307,28 @@
 
         return c
 
-    lax.fori_loop(gone, tiles, late, 0)
-    done = (tiles - take_at) * 3
-    second_leg(tiles - 2)
-    second_leg(tiles - 1)
-
+    stop = tiles - 1 - lead
+    lax.fori_loop(next_two, stop, late, 0)
+    first_leg(None, 0)
+    first_leg(None, 1)
+
+    def finish_to(lo, hi):
+        def body(r, c):
+            finish_round(r)
+            return c
+
+        lax.fori_loop(lo, hi, body, 0)
+
+    def ending(k, c):
+        second_leg(k)
+        finish_round((k - stop) * 2 + (stop - take_at) * 3)
+        finish_round((k - stop) * 2 + (stop - take_at) * 3 + 1)
+        return c
+
+    lax.fori_loop(stop, tiles - 1, ending, 0)
+    second_leg(None, 0)
+    second_leg(None, 1)
+    finish_to((stop - take_at) * 3 + lead * 2, tiles - 1)
     pltpu.make_async_copy(tall.at[pl.ds(0, n - 1)], tall.at[pl.ds(0, n - 1)], t_rs).wait()
     own_rows = own_groups * SUB
     lane1 = lax.broadcasted_iota(jnp.int32, (1, LANES), 1)
@@ -313,16 +343,25 @@
     for q in range(rows // LANES):
         pick_ref[q * LANES : (q + 1) * LANES] = acc[q].reshape(LANES)
 
-    def last(r, c):
-        finish_round(r)
-        return c
-
-    lax.fori_loop(done, tiles, last, 0)
+    finish_round(tiles - 1, 0)
+    finish_round(tiles - 1, 1)
 
     pltpu.make_async_copy(mid.at[pl.ds(0, side - 1)], mid.at[pl.ds(0, side - 1)], one_ss).wait()
     pltpu.make_async_copy(recv.at[pl.ds(0, 2 * side - 1)], recv.at[pl.ds(0, 2 * side - 1)], two_ss).wait()
     pltpu.make_async_copy(stat_in.at[pl.ds(0, n - 1)], stat_in.at[pl.ds(0, n - 1)], stat_ss).wait()
     pltpu.make_async_copy(tall.at[pl.ds(0, n - 1)], tall.at[pl.ds(0, n - 1)], t_ss).wait()
+
+
+def store_kernel(table, picked, table_out, picked_out, sem, small_sem):
+    width = table.shape[1] // STORES
+    copies = [pltpu.make_async_copy(picked, picked_out, small_sem)]
+    for i in range(STORES):
+        cols = pl.ds(i * width, width)
+        copies.append(pltpu.make_async_copy(table.at[:, cols], table_out.at[:, cols], sem.at[i]))
+    for copy in copies:
+        copy.start()
+    for copy in copies:
+        copy.wait()
 
 
 def solution(mesh):
@@ -340,7 +379,7 @@
             functools.partial(kernel, n),
             out_shape=(
                 pltpu.VMEM((own_rows, n * local_vocab), f32),
-                jax.ShapeDtypeStruct((rows,), f32),
+                pltpu.VMEM((rows,), f32),
             ),
             in_specs=[
                 pl.BlockSpec(memory_space=pltpu.HBM),
@@ -363,16 +402,16 @@
                 pltpu.VMEM((n, SUB, LANES), f32),
                 pltpu.VMEM((own_rows // SUB, n, SUB, LANES), f32),
                 pltpu.VMEM((own_rows // SUB, n, SUB, LANES), f32),
-                pltpu.VMEM((tiles, own_rows // SUB, n, SUB, LANES), f32),
-                pltpu.VMEM((tiles, own_rows // SUB, n, SUB, LANES), f32),
+                pltpu.VMEM((own_rows // SUB, n, SUB, LANES), f32),
+                pltpu.VMEM((own_rows // SUB, n, SUB, LANES), f32),
                 pltpu.VMEM((1, LANES), f32),
                 pltpu.VMEM((n, 1, LANES), f32),
                 pltpu.SemaphoreType.DMA,
                 pltpu.SemaphoreType.DMA((SLOTS,)),
                 pltpu.SemaphoreType.DMA,
-                pltpu.SemaphoreType.DMA((tiles,)),
-                pltpu.SemaphoreType.DMA,
-                pltpu.SemaphoreType.DMA((tiles,)),
+                pltpu.SemaphoreType.DMA((tiles + 1,)),
+                pltpu.SemaphoreType.DMA,
+                pltpu.SemaphoreType.DMA((tiles + 1,)),
                 pltpu.SemaphoreType.DMA,
                 pltpu.SemaphoreType.DMA,
                 pltpu.SemaphoreType.DMA,
@@ -381,7 +420,18 @@
             compiler_params=pltpu.CompilerParams(collective_id=0, has_side_effects=True, vmem_limit_bytes=54 << 20),
             name="head_cdf",
         )(hidden, w_local, inv_temp, target_ids)
-        return table, picked
+        return pl.pallas_call(
+            store_kernel,
+            out_shape=(
+                jax.ShapeDtypeStruct(table.shape, f32),
+                jax.ShapeDtypeStruct(picked.shape, f32),
+            ),
+            in_specs=[pl.BlockSpec(memory_space=pltpu.VMEM)] * 2,
+            out_specs=(pl.BlockSpec(memory_space=pltpu.HBM), pl.BlockSpec(memory_space=pltpu.HBM)),
+            scratch_shapes=[pltpu.SemaphoreType.DMA((STORES,)), pltpu.SemaphoreType.DMA],
+            compiler_params=pltpu.CompilerParams(vmem_limit_bytes=20 << 20),
+            name="store_table",
+        )(table, picked)
 
     return jax.shard_map(
         local_step,

time: 97.6 us -> 93.1 us (0.954)
  local copies, waits for them, and re-layouts: 3.98 us -> 0 us
    unnamed x4 -> x0, local copies, waits for them, and re-layouts: 3.98 us -> none
    pallas_call x1, Pallas kernels: 92.8 us -> 89 us  [local_step(): pl.pallas_call(functools.partial(kernel, n), out_shape=(pltpu.VMEM((own_r...]
    pallas_call x0 -> x1, Pallas kernels: none -> 3.38 us  [local_step(): pl.pallas_call(store_kernel, out_shape=(jax.ShapeDtypeStruct(table.shape,...]
where the time goes in v4:
time: 93.1 us; the launch traced here: 93 us
  Pallas kernels  92.4 us (99%)
    pallas_call x1, Pallas kernels, local_step(): pl.pallas_call(functools.partial(kernel, n), out_shape=(pltpu.VMEM((own_r...  89 us
    pallas_call x1, Pallas kernels, local_step(): pl.pallas_call(store_kernel, out_shape=(jax.ShapeDtypeStruct(table.shape,...  3.38 us

profile of v4, /device:TPU:97, one launch (start us, length us, event | category | flops | bytes accessed | tf_op | source)
XLA Modules:
  0.0 93.0 jit_solution(4617276456167754758)
XLA Ops:
  0.6 89.0 %head_cdf.1 = (f32[12,131072]{1,0:T(8,128)S(1)}, f32[384]{0:T(512)S(1)}) custom-call(bf16[384,5120]{1,0:T(8,128)(2,1)} %hid_hbm.1, bf16[5120,4096]{1,0:T(8,128)(2,1)} %w_hbm.1, f32[384]{0:T(512)} %inv_ref.1, s32[384]{0:T(512)} %tgt_ref.1), custom_call_target="tpu_custom_call" | custom-call | tf_op jit(solution)/shard_map/head_cdf/pallas_call | solution.py:378
  89.6 3.4 %store_table.1 = (f32[12,131072]{1,0:T(8,128)}, f32[384]{0:T(512)}) custom-call(f32[12,131072]{1,0:T(8,128)S(1)} %get-tuple-element.4.table, f32[384]{0:T(512)S(1)} %get-tuple-element.5.picked), custom_call_target="tpu_custom_call" | custom-call | tf_op jit(solution)/shard_map/store_table/pallas_call | solution.py:423

commit v5 on v4

--- a/solution.py
+++ b/solution.py
@@ -15,6 +15,7 @@
 HALF = TILE // 2
 SLOTS = 3
 PARTS = 4
+AHEAD = 4
 STORES = 8
 LOW = -3.0e38
 
@@ -269,26 +270,27 @@
             pl.semaphore_wait(barrier, n - 1)
             first_leg(t)
 
-        @pl.when(t == 1)
+        @pl.when((t >= 1) & (t < AHEAD))
         def _():
             first_leg(t)
 
-        @pl.when((t >= 2) & (t % 2 == 0))
-        def _():
-            first_leg(t // 2 + 1)
-
-        @pl.when((t >= 3) & (t % 2 == 1))
-        def _():
-            second_leg((t - 3) // 2)
+        @pl.when((t >= AHEAD) & ((t - AHEAD) % 2 == 1))
+        def _():
+            first_leg(AHEAD + (t - AHEAD) // 2)
+
+        @pl.when((t >= AHEAD + 2) & ((t - AHEAD) % 2 == 0))
+        def _():
+            second_leg((t - AHEAD) // 2 - 1)
 
         return c
 
     lax.fori_loop(0, tiles, early, 0)
     send_statistics()
 
-    next_one, next_two = tiles // 2 + 1, tiles // 2 - 1
-    first_leg(jnp.int32(next_one))
-    lead = next_one + 1 - next_two
+    lead = AHEAD + 1
+    next_one, next_two = AHEAD + (tiles - AHEAD) // 2, (tiles - 1 - AHEAD) // 2
+    for k in range(next_one, next_two + lead):
+        first_leg(jnp.int32(k))
     take_at = next_two + 3
 
     def late(k, c):
@@ -319,16 +321,17 @@
 
         lax.fori_loop(lo, hi, body, 0)
 
+    ready = (stop - take_at) * 3
+
     def ending(k, c):
         second_leg(k)
-        finish_round((k - stop) * 2 + (stop - take_at) * 3)
-        finish_round((k - stop) * 2 + (stop - take_at) * 3 + 1)
+        finish_round(k - stop + ready)
         return c
 
     lax.fori_loop(stop, tiles - 1, ending, 0)
     second_leg(None, 0)
     second_leg(None, 1)
-    finish_to((stop - take_at) * 3 + lead * 2, tiles - 1)
+    finish_to(tiles - 1 - stop + ready, tiles - 1)
     pltpu.make_async_copy(tall.at[pl.ds(0, n - 1)], tall.at[pl.ds(0, n - 1)], t_rs).wait()
     own_rows = own_groups * SUB
     lane1 = lax.broadcasted_iota(jnp.int32, (1, LANES), 1)
@@ -357,7 +360,8 @@
     copies = [pltpu.make_async_copy(picked, picked_out, small_sem)]
     for i in range(STORES):
         cols = pl.ds(i * width, width)
-        copies.append(pltpu.make_async_copy(table.at[:, cols], table_out.at[:, cols], sem.at[i]))
+        for k, rows in enumerate((pl.ds(0, 8), pl.ds(8, table.shape[0] - 8))):
+            copies.append(pltpu.make_async_copy(table.at[rows, cols], table_out.at[rows, cols], sem.at[i, k]))
     for copy in copies:
         copy.start()
     for copy in copies:
@@ -428,7 +432,7 @@
             ),
             in_specs=[pl.BlockSpec(memory_space=pltpu.VMEM)] * 2,
             out_specs=(pl.BlockSpec(memory_space=pltpu.HBM), pl.BlockSpec(memory_space=pltpu.HBM)),
-            scratch_shapes=[pltpu.SemaphoreType.DMA((STORES,)), pltpu.SemaphoreType.DMA],
+            scratch_shapes=[pltpu.SemaphoreType.DMA((STORES, 2)), pltpu.SemaphoreType.DMA],
             compiler_params=pltpu.CompilerParams(vmem_limit_bytes=20 << 20),
             name="store_table",
         )(table, picked)

time: 93.1 us -> 94.4 us (1.014)
  Pallas kernels: 92.4 us -> 93.7 us
    pallas_call x1, Pallas kernels: 89 us -> 90.2 us  [local_step(): pl.pallas_call(functools.partial(kernel, n), out_shape=(pltpu.VMEM((own_r...]
where the time goes in v5:
time: 94.4 us; the launch traced here: 94.3 us
  Pallas kernels  93.7 us (99%)
    pallas_call x1, Pallas kernels, local_step(): pl.pallas_call(functools.partial(kernel, n), out_shape=(pltpu.VMEM((own_r...  90.2 us
    pallas_call x1, Pallas kernels, local_step(): pl.pallas_call(store_kernel, out_shape=(jax.ShapeDtypeStruct(table.shape,...  3.43 us

profile of v5, /device:TPU:97, one launch (start us, length us, event | category | flops | bytes accessed | tf_op | source)
XLA Modules:
  0.0 94.3 jit_solution(6065937112751144300)
XLA Ops:
  0.6 90.2 %head_cdf.1 = (f32[12,131072]{1,0:T(8,128)S(1)}, f32[384]{0:T(512)S(1)}) custom-call(bf16[384,5120]{1,0:T(8,128)(2,1)} %hid_hbm.1, bf16[5120,4096]{1,0:T(8,128)(2,1)} %w_hbm.1, f32[384]{0:T(512)} %inv_ref.1, s32[384]{0:T(512)} %tgt_ref.1), custom_call_target="tpu_custom_call" | custom-call | tf_op jit(solution)/shard_map/head_cdf/pallas_call | solution.py:382
  90.9 3.4 %store_table.1 = (f32[12,131072]{1,0:T(8,128)}, f32[384]{0:T(512)}) custom-call(f32[12,131072]{1,0:T(8,128)S(1)} %get-tuple-element.4.table, f32[384]{0:T(512)S(1)} %get-tuple-element.5.picked), custom_call_target="tpu_custom_call" | custom-call | tf_op jit(solution)/shard_map/store_table/pallas_call | solution.py:427

commit v6 on v4

--- a/solution.py
+++ b/solution.py
@@ -20,7 +20,7 @@
 
 
 def kernel(n, hid_hbm, w_hbm, inv_ref, tgt_ref, out_ref, pick_ref, hid, wbuf, send, mid, recv, invcol, tcol, tri, stat,
-           stat_out, stat_in, scale, offset, scale_b, offset_b, tval, tall, hsem, wsem, one_ss, one_rs, two_ss, two_rs,
+           stat_out, stat_in, scale, offset, scale_b, offset_b, tval, tall, hsem, fsem, wsem, one_ss, one_rs, two_ss, two_rs,
            stat_ss, stat_rs, t_ss, t_rs):
     me = lax.axis_index("vp")
     rows, depth = hid.shape
@@ -46,10 +46,19 @@
             part = pl.ds(p * (depth // PARTS), depth // PARTS)
             pltpu.make_async_copy(w_hbm.at[part, cols], wbuf.at[t % SLOTS, part], wsem.at[t % SLOTS]).start()
 
+    def depth_part(p):
+        return pl.ds(p * (depth // PARTS), depth // PARTS)
+
+    def first_loads(p):
+        part = depth_part(p)
+        return (
+            pltpu.make_async_copy(hid_hbm.at[:, part], hid.at[:, part], hsem.at[p]),
+            pltpu.make_async_copy(w_hbm.at[part, pl.ds(0, TILE)], wbuf.at[0, part], fsem.at[p]),
+        )
+
     for p in range(PARTS):
-        part = pl.ds(p * (rows // PARTS), rows // PARTS)
-        pltpu.make_async_copy(hid_hbm.at[part], hid.at[part], hsem).start()
-    w_start(jnp.int32(0))
+        for copy in first_loads(p):
+            copy.start()
 
     barrier = pltpu.get_barrier_semaphore()
 
@@ -113,18 +122,25 @@
         onward(b, 1 - core)
         recv[core * side + b, :, :, :, cols] = mid[:, pl.ds((b * 2 + core) * own_groups, own_groups), :, cols]
 
-    def compute_tile(t):
-        pltpu.make_async_copy(wbuf.at[t % SLOTS], wbuf.at[t % SLOTS], wsem.at[t % SLOTS]).wait()
-
-        @pl.when(t == 0)
-        def _():
-            w_start(t + 1)
-
-        @pl.when(t + 2 < tiles)
-        def _():
-            w_start(t + 2)
-
-        z = jnp.dot(hid[...], wbuf[t % SLOTS], preferred_element_type=jnp.float32)
+    def compute_tile(t, send_now=None):
+        if send_now:
+            z = None
+            for p in range(PARTS):
+                for copy in first_loads(p):
+                    copy.wait()
+                if p == PARTS - 1:
+                    w_start(jnp.int32(1))
+                    w_start(jnp.int32(2))
+                term = jnp.dot(hid[:, depth_part(p)], wbuf[0, depth_part(p)], preferred_element_type=jnp.float32)
+                z = term if z is None else z + term
+        else:
+            pltpu.make_async_copy(wbuf.at[t % SLOTS], wbuf.at[t % SLOTS], wsem.at[t % SLOTS]).wait()
+
+            @pl.when(t + 2 < tiles)
+            def _():
+                w_start(t + 2)
+
+            z = jnp.dot(hid[...], wbuf[t % SLOTS], preferred_element_type=jnp.float32)
         z = z * jnp.concatenate([invcol[...]] * (TILE // LANES), axis=1)
         top = jnp.max(z, axis=1, keepdims=True)
         e = jnp.exp(z - top)
@@ -142,6 +158,9 @@
             oy, ox, oc = owner // (2 * side), (owner // 2) % side, owner % 2
             x_first, y_first = ((ox * side + oy) * 2 + oc) * own_groups + g, ((oy * side + ox) * 2 + oc) * own_groups + g
             send[x_first + core * (y_first - x_first), :, cols] = run[k * SUB : (k + 1) * SUB]
+        mid[a, :, :, cols] = send[pl.ds(a * slab, slab), :, cols]
+        if send_now:
+            send_now()
         at = lax.broadcasted_iota(jnp.int32, (rows, TILE), 1).astype(jnp.float32) + (t * TILE).astype(jnp.float32)
         tc = jnp.concatenate([tcol[...]] * (TILE // LANES), axis=1)
         hit = jnp.sum(jnp.where(at == tc, run, 0.0), axis=1, keepdims=True)
@@ -151,7 +170,6 @@
         st = jnp.where(lane == tiles + t, run[:, TILE - 1 :], st)
         st = jnp.where(lane == 2 * tiles, st + hit, st)
         stat[...] = st
-        mid[a, :, :, cols] = send[pl.ds(a * slab, slab), :, cols]
 
     def send_statistics():
         lane8 = lax.broadcasted_iota(jnp.int32, (rows, LANES), 1)
@@ -259,15 +277,14 @@
 
         lax.fori_loop(0, n, one, 0, unroll=4)
 
-    pltpu.make_async_copy(hid, hid, hsem).wait()
+    def first_send():
+        pl.semaphore_wait(barrier, n - 1)
+        first_leg(jnp.int32(0))
+
+    compute_tile(jnp.int32(0), first_send)
 
     def early(t, c):
         compute_tile(t)
-
-        @pl.when(t == 0)
-        def _():
-            pl.semaphore_wait(barrier, n - 1)
-            first_leg(t)
 
         @pl.when(t == 1)
         def _():
@@ -283,7 +300,7 @@
 
         return c
 
-    lax.fori_loop(0, tiles, early, 0)
+    lax.fori_loop(1, tiles, early, 0)
     send_statistics()
 
     next_one, next_two = tiles // 2 + 1, tiles // 2 - 1
@@ -406,7 +423,8 @@
                 pltpu.VMEM((own_rows // SUB, n, SUB, LANES), f32),
                 pltpu.VMEM((1, LANES), f32),
                 pltpu.VMEM((n, 1, LANES), f32),
-                pltpu.SemaphoreType.DMA,
+                pltpu.SemaphoreType.DMA((PARTS,)),
+                pltpu.SemaphoreType.DMA((PARTS,)),
                 pltpu.SemaphoreType.DMA((SLOTS,)),
                 pltpu.SemaphoreType.DMA,
                 pltpu.SemaphoreType.DMA((tiles + 1,)),

time: 93.1 us -> 92.5 us (level)
  no operation moved by 1% of the time
where the time goes in v6:
time: 92.5 us; the launch traced here: 92.4 us
  Pallas kernels  91.8 us (99%)
    pallas_call x1, Pallas kernels, local_step(): pl.pallas_call(functools.partial(kernel, n), out_shape=(pltpu.VMEM((own_r...  88.4 us
    pallas_call x1, Pallas kernels, local_step(): pl.pallas_call(store_kernel, out_shape=(jax.ShapeDtypeStruct(table.shape,...  3.38 us

profile of v6, /device:TPU:97, one launch (start us, length us, event | category | flops | bytes accessed | tf_op | source)
XLA Modules:
  0.0 92.4 jit_solution(1008965538626465181)
XLA Ops:
  0.6 88.4 %head_cdf.1 = (f32[12,131072]{1,0:T(8,128)S(1)}, f32[384]{0:T(512)S(1)}) custom-call(bf16[384,5120]{1,0:T(8,128)(2,1)} %hid_hbm.1, bf16[5120,4096]{1,0:T(8,128)(2,1)} %w_hbm.1, f32[384]{0:T(512)} %inv_ref.1, s32[384]{0:T(512)} %tgt_ref.1), custom_call_target="tpu_custom_call" | custom-call | tf_op jit(solution)/shard_map/head_cdf/pallas_call | solution.py:395
  89.0 3.4 %store_table.1 = (f32[12,131072]{1,0:T(8,128)}, f32[384]{0:T(512)}) custom-call(f32[12,131072]{1,0:T(8,128)S(1)} %get-tuple-element.4.table, f32[384]{0:T(512)S(1)} %get-tuple-element.5.picked), custom_call_target="tpu_custom_call" | custom-call | tf_op jit(solution)/shard_map/store_table/pallas_call | solution.py:441

commit v7 on v6

--- a/solution.py
+++ b/solution.py
@@ -286,17 +286,13 @@
     def early(t, c):
         compute_tile(t)
 
-        @pl.when(t == 1)
+        @pl.when(t % 2 == 1)
         def _():
-            first_leg(t)
-
-        @pl.when((t >= 2) & (t % 2 == 0))
+            first_leg((t + 1) // 2)
+
+        @pl.when(t % 2 == 0)
         def _():
-            first_leg(t // 2 + 1)
-
-        @pl.when((t >= 3) & (t % 2 == 1))
-        def _():
-            second_leg((t - 3) // 2)
+            second_leg(t // 2 - 1)
 
         return c
 

time: 92.5 us -> 95.9 us (1.037)
  Pallas kernels: 91.8 us -> 95.2 us
    pallas_call x1, Pallas kernels: 88.4 us -> 91.8 us  [local_step(): pl.pallas_call(functools.partial(kernel, n), out_shape=(pltpu.VMEM((own_r...]
where the time goes in v7:
time: 95.9 us; the launch traced here: 95.8 us
  Pallas kernels  95.2 us (99%)
    pallas_call x1, Pallas kernels, local_step(): pl.pallas_call(functools.partial(kernel, n), out_shape=(pltpu.VMEM((own_r...  91.8 us
    pallas_call x1, Pallas kernels, local_step(): pl.pallas_call(store_kernel, out_shape=(jax.ShapeDtypeStruct(table.shape,...  3.38 us

profile of v7, /device:TPU:97, one launch (start us, length us, event | category | flops | bytes accessed | tf_op | source)
XLA Modules:
  0.0 95.8 jit_solution(7179828576641627766)
XLA Ops:
  0.6 91.8 %head_cdf.1 = (f32[12,131072]{1,0:T(8,128)S(1)}, f32[384]{0:T(512)S(1)}) custom-call(bf16[384,5120]{1,0:T(8,128)(2,1)} %hid_hbm.1, bf16[5120,4096]{1,0:T(8,128)(2,1)} %w_hbm.1, f32[384]{0:T(512)} %inv_ref.1, s32[384]{0:T(512)} %tgt_ref.1), custom_call_target="tpu_custom_call" | custom-call | tf_op jit(solution)/shard_map/head_cdf/pallas_call | solution.py:391
  92.4 3.4 %store_table.1 = (f32[12,131072]{1,0:T(8,128)}, f32[384]{0:T(512)}) custom-call(f32[12,131072]{1,0:T(8,128)S(1)} %get-tuple-element.4.table, f32[384]{0:T(512)S(1)} %get-tuple-element.5.picked), custom_call_target="tpu_custom_call" | custom-call | tf_op jit(solution)/shard_map/store_table/pallas_call | solution.py:437
